TPU v7x, 32 devices: a whole 2x2x4 slice. The times are simulated.
32 devices in a mesh: grp: 2 (over x), patch: 16 (over z, y, core).
Axes of the slice: x: 2, y: 2, z: 4, core: 2. Of those that a mesh axis runs over, the one named last changes fastest.
Arguments:
- features: bfloat16 [4, 16, 32, 640], P('grp', 'patch'), parts along dimension 0, may hold values from -6 to 6
- stale_conv_in: bfloat16 [4, 16, 32, 640], P('grp', 'patch'), parts along dimension 0, may hold values from -4.1875 to 4.1875
- stale_normed: bfloat16 [4, 16, 32, 640], P('grp', 'patch'), parts along dimension 0, may hold values from -6 to 6
- first_gain: float32 [640], replicated, may hold values from 0.1 to 1.9
- first_bias: float32 [640], replicated, may hold values from -1.8 to 1.8
- conv_weight: bfloat16 [3, 3, 640, 640], replicated, may hold values from -0.078125 to 0.078125
- conv_bias: float32 [640], replicated, may hold values from -1.8 to 1.8
- second_gain: float32 [640], replicated, may hold values from 0.1 to 1.9
- second_bias: float32 [640], replicated, may hold values from -1.8 to 1.8
- query_weight: bfloat16 [640, 640], replicated, may hold values from -6 to 6
- key_weight: bfloat16 [640, 640], replicated, may hold values from -6 to 6
- value_weight: bfloat16 [640, 640], replicated, may hold values from -0.25 to 0.25
- output_weight: bfloat16 [640, 640], replicated, may hold values from -0.25 to 0.25
- layer_gain: float32 [640], replicated, may hold values from 0.1 to 1.9
- cross_query: bfloat16 [640, 640], replicated, may hold values from -0.5 to 0.5
- cross_output: bfloat16 [640, 640], replicated, may hold values from -0.25 to 0.25
- text_keys: bfloat16 [4, 77, 640], P('grp'), parts along dimension 0, may hold values from -32 to 32
- text_values: bfloat16 [4, 77, 640], P('grp'), parts along dimension 0, may hold values from -6 to 6
Outputs:
- block_output: float32 [4, 16, 32, 640], P('grp', 'patch'), parts along dimension 0
There are 2 independent parts, one for each index of `grp`. A program takes and returns all parts, laid end to end along the dimension named above; an argument that names none is the same for every part. Nothing has to cross between parts.
All inputs are finite; a program needn't handle non-finite values.
Results may differ from a plain program's by a relative error of at most 0.02.
The roundings to bfloat16 on the way count: a program that leaves them out, or rounds other values in their place, can miss the bound.
Values may be sent and summed in bfloat16 or wider, within the bound.
A program may use at most 128 MiB of HBM per device.

v0:
```python
import jax
import jax.numpy as jnp
from jax import lax
from jax.sharding import PartitionSpec as P

GROUPS = 32
HEADS = 10
HEAD_DIM = 64
CTX = 77


EPSILON = 1e-05
NEG_LARGE = -1e30


def from_partner(value, axis, apart):
    return lax.ppermute(value, axis, [(i, i ^ 1 << apart) for i in range(lax.axis_size(axis))])


def shifted(value, axis, steps):
    count = lax.axis_size(axis)
    initial, last = (max(0, -steps), min(count, count - steps))
    return lax.ppermute(value, axis, [(source, source + steps) for source in range(initial, last)])


def project(values, weight):
    return jnp.dot(values, weight, preferred_element_type=jnp.float32).astype(jnp.bfloat16)


def group_norm(features, scale_vec, shift_vec):
    images, patches, columns, channels = features.shape
    group_width = channels // GROUPS
    total_count = lax.axis_size("patch") * patches * columns * group_width
    grouped = features.astype(jnp.float32).reshape(images, patches, columns, GROUPS, group_width)
    sum_values, sum_squares = lax.psum(
        (jnp.sum(grouped, axis=(1, 2, 4)), jnp.sum(grouped * grouped, axis=(1, 2, 4))), "patch"
    )
    group_mean = sum_values / total_count
    group_var = sum_squares / total_count - group_mean * group_mean
    group_mean = group_mean[:, None, None, :, None]
    group_var = group_var[:, None, None, :, None]
    normed = ((grouped - group_mean) * lax.rsqrt(group_var + EPSILON)).reshape(features.shape)
    return normed * scale_vec + shift_vec


def layer_norm(values, scale_vec):
    layer_mean = jnp.mean(values, axis=-1, keepdims=True)
    centred = values - layer_mean
    layer_var = jnp.mean(centred * centred, axis=-1, keepdims=True)
    return centred * lax.rsqrt(layer_var + EPSILON) * scale_vec


def patch_conv(fresh, stale, conv_weight):
    images = fresh.shape[0]
    columns = fresh.shape[2]
    channels = fresh.shape[3]
    position = lax.axis_index("patch")
    right_side = position % 2 == 1
    edge_column = jnp.where(right_side, stale[:, :, :1], stale[:, :, -1:])
    across = from_partner(edge_column, "patch", 0)
    zeros_column = jnp.zeros_like(across)
    left_column = jnp.where(right_side, across, zeros_column)
    right_column = jnp.where(right_side, zeros_column, across)
    stale_wide = jnp.concatenate([left_column, stale, right_column], axis=2)
    fresh_wide = jnp.concatenate([left_column, fresh, right_column], axis=2)
    above = shifted(stale_wide, "patch", 2)
    below = shifted(stale_wide, "patch", -2)
    window = jnp.concatenate([above, fresh_wide, below], axis=1)
    taps = jnp.concatenate(
        [
            window[:, offset_row, offset_col : offset_col + columns]
            for offset_row in range(3)
            for offset_col in range(3)
        ],
        axis=-1,
    )
    flat = jnp.dot(
        taps.reshape(images * columns, 9 * channels),
        conv_weight.reshape(9 * channels, channels),
        preferred_element_type=jnp.float32,
    )
    return flat.reshape(images, 1, columns, channels)


def attend(carry, queries, keys, values, scale):
    maxima, totals, accumulated = carry
    scores = (
        jnp.einsum("bqhd,bkhd->bhqk", queries, keys, preferred_element_type=jnp.float32) * scale
    )
    new_max = jnp.maximum(maxima, jnp.max(scores, axis=-1))
    weights = jnp.exp(scores - new_max[..., None])
    fading = jnp.exp(maxima - new_max)
    totals = totals * fading + jnp.sum(weights, axis=-1)
    update = jnp.einsum(
        "bhqk,bkhd->bhqd", weights.astype(jnp.bfloat16), values, preferred_element_type=jnp.float32
    )
    accumulated = accumulated * fading[..., None] + update
    return (new_max, totals, accumulated)


def blocked(carry, pieces, start, handle):
    span = pieces[0].shape[1]
    limit = min(span, 16)
    divisor = max((candidate for candidate in range(1, limit + 1) if span % candidate == 0))
    count = span // divisor
    if count == 1:
        return handle(carry, pieces, start)

    def advance(index, state):
        cut = tuple(
            (lax.dynamic_slice_in_dim(item, index * divisor, divisor, 1) for item in pieces)
        )
        return handle(state, cut, start + index * divisor)

    return lax.fori_loop(0, count, advance, carry)


def on_device(
    features,
    stale_conv_in,
    stale_normed,
    first_gain,
    first_bias,
    conv_weight,
    conv_bias,
    second_gain,
    second_bias,
    query_weight,
    key_weight,
    value_weight,
    output_weight,
    layer_gain,
    cross_query,
    cross_output,
    text_keys,
    text_values,
):
    images = features.shape[0]
    columns = features.shape[2]
    channels = features.shape[3]
    width = HEADS * HEAD_DIM
    scale = HEAD_DIM ** (-0.5)
    conv_input = jax.nn.silu(group_norm(features, first_gain, first_bias)).astype(jnp.bfloat16)
    conv_out = patch_conv(conv_input, stale_conv_in, conv_weight)
    hidden = features.astype(jnp.float32) + conv_out + conv_bias
    attn_input = group_norm(hidden, second_gain, second_bias).astype(jnp.bfloat16)
    flat_input = attn_input.reshape(images * columns, channels)
    queries = project(flat_input, query_weight).reshape(images, columns, HEADS, HEAD_DIM)
    fresh_keys = project(flat_input, key_weight).reshape(images, 1, columns, width)
    fresh_values = project(flat_input, value_weight).reshape(images, 1, columns, width)
    position = lax.axis_index("patch")

    def fold_pair(carry, pieces, start):
        piece_keys, piece_values = pieces
        span = piece_keys.shape[1]
        mine = start + jnp.arange(span, dtype=jnp.int32) == position
        piece_keys = jnp.where(mine[None, :, None, None], fresh_keys, piece_keys)
        piece_values = jnp.where(mine[None, :, None, None], fresh_values, piece_values)
        flat_keys = piece_keys.reshape(images, span * columns, HEADS, HEAD_DIM)
        flat_values = piece_values.reshape(images, span * columns, HEADS, HEAD_DIM)
        return attend(carry, queries, flat_keys, flat_values, scale)

    initial = (
        jnp.full((images, HEADS, columns), NEG_LARGE, jnp.float32),
        jnp.zeros((images, HEADS, columns), jnp.float32),
        jnp.zeros((images, HEADS, columns, HEAD_DIM), jnp.float32),
    )

    def fold_inputs(carry, pieces, start):
        piece = pieces[0]
        span = piece.shape[1]
        piece_flat = piece.reshape(images * span * columns, channels)
        piece_keys = project(piece_flat, key_weight).reshape(images, span, columns, width)
        piece_values = project(piece_flat, value_weight).reshape(images, span, columns, width)
        return fold_pair(carry, (piece_keys, piece_values), start)

    final = blocked(
        initial,
        (lax.all_gather(stale_normed, "patch", axis=1, tiled=True),),
        jnp.int32(0),
        fold_inputs,
    )
    unused_max, totals, accumulated = final
    attended = (
        (accumulated / totals[..., None])
        .transpose(0, 2, 1, 3)
        .reshape(images * columns, width)
        .astype(jnp.bfloat16)
    )
    mixed = hidden.reshape(images * columns, channels) + jnp.dot(
        attended, output_weight, preferred_element_type=jnp.float32
    )
    layer_in = layer_norm(mixed, layer_gain).astype(jnp.bfloat16)
    cross_q = project(layer_in, cross_query).reshape(images, columns, HEADS, HEAD_DIM)
    text_k = text_keys.reshape(images, CTX, HEADS, HEAD_DIM)
    text_v = text_values.reshape(images, CTX, HEADS, HEAD_DIM)
    cross_scores = (
        jnp.einsum("bqhd,bkhd->bhqk", cross_q, text_k, preferred_element_type=jnp.float32) * scale
    )
    cross_max = jnp.max(cross_scores, axis=-1, keepdims=True)
    cross_weights = jnp.exp(cross_scores - cross_max)
    cross_totals = jnp.sum(cross_weights, axis=-1)
    cross_numer = jnp.einsum(
        "bhqk,bkhd->bhqd",
        cross_weights.astype(jnp.bfloat16),
        text_v,
        preferred_element_type=jnp.float32,
    )
    cross_attn = (
        (cross_numer / cross_totals[..., None])
        .transpose(0, 2, 1, 3)
        .reshape(images * columns, width)
        .astype(jnp.bfloat16)
    )
    block_output = mixed + jnp.dot(cross_attn, cross_output, preferred_element_type=jnp.float32)
    return block_output.reshape(images, 1, columns, channels)


def solution(mesh):
    in_specs = (
        P("grp", "patch", None, None),
        P("grp", "patch", None, None),
        P("grp", "patch", None, None),
        P(),
        P(),
        P(),
        P(),
        P(),
        P(),
        P(),
        P(),
        P(),
        P(),
        P(),
        P(),
        P(),
        P("grp", None, None),
        P("grp", None, None),
    )
    out_specs = P("grp", "patch", None, None)
    return jax.shard_map(
        on_device, mesh=mesh, in_specs=in_specs, out_specs=out_specs, check_vma=False
    )
```

profile of v0, /device:TPU:1, one launch (start us, length us, event | category | flops | bytes accessed | tf_op | source)
XLA Modules:
  0.0 136.6 jit_solution(12319141725540506762)
XLA Ops:
  6.6 0.8 broadcast_select_fusion.4
  7.6 0.9 convert_reduce_fusion
  8.5 0.1 reduce_sum.106
  8.6 0.1 reduce_sum.83
  8.9 30.7 %all-reduce.1 = (f32[2,32]{1,0:T(2,128)S(1)}, f32[2,32]{1,0:T(2,128)S(1)}) all-reduce(f32[2,32]{1,0:T(2,128)S(1)} %reduce_sum.107, f32[2,32]{1,0:T(2,128)S(1)} %reduce_sum.84), channel_id=1, replica_groups=mesh['grp'=2,'patch'=16] {'patch'}, use_global_device_ids=true, to_apply=%region_5.6 | all-reduce | flops 128 | bytes 1024 | tf_op jit(solution)/shard_map/psum | solution.py:35
  39.7 0.1 mul.115
  39.9 0.1 sub.76
  40.0 1.0 fusion.38
  41.0 0.9 pad_maximum_fusion
  41.9 1.3 collective-permute-start.1
  43.3 0.1 broadcast_in_dim.68
  43.4 1.2 copy.44
  44.6 1.9 %copy.46 = bf16[2,77,640]{1,2,0:T(8,128)(2,1)} copy(bf16[2,77,640]{2,0,1:T(2,128)(2,1)} %param.35) | data formatting | bytes 394240 | tf_op args[17]
  46.4 1.3 collective-permute-start.2
  48.0 3.8 %collective-permute-done.2 = bf16[2,1,34,640]{3,2,0,1:T(8,128)(2,1)S(1)} collective-permute-done((bf16[2,1,34,640]{3,2,0,1:T(8,128)(2,1)S(1)}, bf16[2,1,34,640]{3,2,0,1:T(8,128)(2,1)S(1)}, u32[]{:S(2)}, u32[]{:S(2)}) %collective-permute-start.2) | collective-permute-done | bytes 87072 | tf_op jit(solution)/shard_map/ppermute | solution.py:23
  52.0 4.5 %fusion.49 = (f32[2,640]{1,0:T(2,128)S(1)}, f32[2,640]{1,0:T(2,128)S(1)}, f32[2,1,32,640]{3,2,0,1:T(8,128)S(1)}) fusion(f32[640]{0:T(1024)S(1)} %copy-done.11, bf16[5760,640,1]{1,0,2:T(8,128)(2,1)} %bitcast.77, bf16[2,1,32,5760]{3,2,0,1:T(8,128)(2,1)S(1)} %slice_dynamic-update-slice_fusion, bf16[2,1,32,640]{3,2,1,0:T(8,128)(2,1)S(1)} %copy-done.1), kind=kOutput, calls=%fused_computation.82 | convolution fusion | flops 472102400 | bytes 8368640 | tf_op jit(solution)/shard_map/dot_general | solution.py:77
  56.5 0.1 reduce_sum.109
  56.7 0.1 reduce_sum.112
  56.9 35.3 %all-reduce = (f32[2,32]{1,0:T(2,128)S(1)}, f32[2,32]{1,0:T(2,128)S(1)}) all-reduce(f32[2,32]{1,0:T(2,128)S(1)} %reduce_sum.113, f32[2,32]{1,0:T(2,128)S(1)} %reduce_sum.110), channel_id=1, replica_groups=mesh['grp'=2,'patch'=16] {'patch'}, use_global_device_ids=true, to_apply=%region_11.12 | all-reduce | flops 128 | bytes 1024 | tf_op jit(solution)/shard_map/psum | solution.py:35
  92.3 0.1 mul.124
  92.5 0.1 sub.81
  92.7 0.3 convolution_convert_fusion.4
  92.9 0.1 broadcast_in_dim.71
  93.1 3.7 %broadcast_in_dim.72 = bf16[2,512,10,64]{3,2,1,0:T(8,128)(2,1)} reshape(bf16[2,16,32,640]{3,2,1,0:T(8,128)(2,1)S(1)} %broadcast_in_dim.71) | data formatting | bytes 2621440 | tf_op jit(solution)/shard_map/jit(_where)/broadcast_in_dim | solution.py:157
  96.8 0.3 convolution_convert_fusion.3
  97.1 0.1 broadcast_in_dim.75
  97.2 3.7 %broadcast_in_dim.76 = bf16[2,512,10,64]{3,2,1,0:T(8,128)(2,1)} reshape(bf16[2,16,32,640]{3,2,1,0:T(8,128)(2,1)S(1)} %broadcast_in_dim.75) | data formatting | bytes 2621440 | tf_op jit(solution)/shard_map/jit(_where)/broadcast_in_dim | solution.py:158
  100.9 0.3 convolution_convert_fusion.5
  101.2 0.2 reshape.202
  101.4 3.9 %convolution_convert_fusion.1 = bf16[1024,640]{1,0:T(8,128)(2,1)} fusion(bf16[1024,640]{1,0:T(8,128)(2,1)} %bitcast.89, bf16[640,640]{1,0:T(8,128)(2,1)S(1)} %copy-done), kind=kOutput, calls=%fused_computation.7 | convolution fusion | flops 839516160 | bytes 3440640 | tf_op jit(solution)/shard_map/dot_general | solution.py:27
  105.3 1.3 convolution_convert_fusion
  106.7 5.8 %reshape.211 = bf16[2,512,10,64]{3,2,1,0:T(8,128)(2,1)} reshape(bf16[1024,640]{1,0:T(8,128)(2,1)} %convolution_convert_fusion.1) | data formatting | bytes 2621440 | tf_op jit(solution)/shard_map/reshape | solution.py:173
  112.5 3.7 %reshape.212 = bf16[2,512,10,64]{3,2,1,0:T(8,128)(2,1)} reshape(bf16[1024,640]{1,0:T(8,128)(2,1)S(1)} %convolution_convert_fusion) | data formatting | bytes 2621440 | tf_op jit(solution)/shard_map/reshape | solution.py:174
  116.2 6.8 %broadcast_select_fusion.1 = (bf16[2,512,10,64]{3,2,1,0:T(8,128)(2,1)S(1)}, bf16[2,512,10,64]{3,2,1,0:T(8,128)(2,1)S(1)}) fusion(bf16[2,512,10,64]{3,2,1,0:T(8,128)(2,1)} %broadcast_in_dim.72, bf16[2,512,10,64]{3,2,1,0:T(8,128)(2,1)} %reshape.211, pred[512]{0:T(512)(128)(4,1)S(1)} %broadcast_in_dim.68, bf16[2,512,10,64]{3,2,1,0:T(8,128)(2,1)} %broadcast_in_dim.76, ...), kind=kLoop, calls=%fused_computation.1 | loop fusion | flops 1310720 | bytes 7864832 | tf_op jit(solution)/shard_map/jit(_where)/select_n | solution.py:157
  123.0 1.2 fusion.50
  124.2 0.4 fusion.21
  124.7 1.2 fusion.18
  126.0 0.2 convert_element_type.63
  126.3 0.4 fusion.51
  126.6 0.2 multiply_reduce_fusion
  126.8 0.2 copy-done.2
  127.1 0.3 convolution_convert_fusion.2
  127.4 0.2 reshape.206
  127.6 0.3 fusion.52
  127.9 0.3 fusion.28
  128.2 0.3 fusion.17
  128.6 0.2 convert_element_type.68
  128.9 0.9 convolution_add_fusion
  (66 shorter events, 1.5 us)
Async XLA Ops:
  6.5 86.1 %copy-start = (bf16[640,640]{1,0:T(8,128)(2,1)S(1)}, bf16[640,640]{1,0:T(8,128)(2,1)}, u32[]{:S(2)}) copy-start(bf16[640,640]{1,0:T(8,128)(2,1)} %param.28) | copy-start | bytes 2457604
  6.5 41.3 %copy-start.1 = (bf16[2,1,32,640]{3,2,1,0:T(8,128)(2,1)S(1)}, bf16[2,1,32,640]{3,2,1,0:T(8,128)(2,1)}, u32[]{:S(2)}) copy-start(bf16[2,1,32,640]{3,2,1,0:T(8,128)(2,1)} %param.18) | copy-start | bytes 245764
  6.5 41.4 %copy-start.10 = (f32[640]{0:T(1024)S(1)}, f32[640]{0:T(1024)}, u32[]{:S(2)}) copy-start(f32[640]{0:T(1024)} %param.21) | copy-start | bytes 7684
  6.5 41.4 %copy-start.9 = (f32[640]{0:T(1024)S(1)}, f32[640]{0:T(1024)}, u32[]{:S(2)}) copy-start(f32[640]{0:T(1024)} %param.22) | copy-start | bytes 7684
  6.5 45.4 %copy-start.11 = (f32[640]{0:T(1024)S(1)}, f32[640]{0:T(1024)}, u32[]{:S(2)}) copy-start(f32[640]{0:T(1024)} %param.24) | copy-start | bytes 7684
  6.5 94.8 %all-gather.2.cloned.1.call-start = ((), (), s32[]{:S(2)}) async-start(), calls=%async_computation | async-start | bytes 1392640 | tf_op jit(solution)/shard_map/all_gather | solution.py:179
  7.5 33.5 %collective-permute-start = (bf16[2,1,1,640]{3,2,0,1:T(2,128)(2,1)S(1)}, bf16[2,1,1,640]{3,2,0,1:T(2,128)(2,1)S(1)}, u32[]{:S(2)}, u32[]{:S(2)}) collective-permute-start(bf16[2,1,1,640]{3,2,0,1:T(2,128)(2,1)S(1)} %broadcast_select_fusion.4), channel_id=1, source_target_pairs={{0,1},{1,0},{2,3},{3,2},{4,5},{5,4},{6,7},{7,6},{8,9},{9,8},{10,11... | collective-permute-start | bytes 7688 | tf_op jit(solution)/shard_map/ppermute | solution.py:17
  41.9 5.8 %collective-permute-start.1 = (bf16[2,1,34,640]{3,2,0,1:T(8,128)(2,1)S(1)}, bf16[2,1,34,640]{3,2,0,1:T(8,128)(2,1)S(1)}, u32[]{:S(2)}, u32[]{:S(2)}) collective-permute-start(bf16[2,1,34,640]{3,2,0,1:T(8,128)(2,1)S(1)} %pad_maximum_fusion), channel_id=1, source_target_pairs={{0,2},{1,3},{2,4},{3,5},{4,6},{5,7},{6,8},{7,9},{8,10},{9,11},{10,... | collective-permute-start | bytes 261128 | tf_op jit(solution)/shard_map/ppermute | solution.py:23
  46.4 5.4 %collective-permute-start.2 = (bf16[2,1,34,640]{3,2,0,1:T(8,128)(2,1)S(1)}, bf16[2,1,34,640]{3,2,0,1:T(8,128)(2,1)S(1)}, u32[]{:S(2)}, u32[]{:S(2)}) collective-permute-start(bf16[2,1,34,640]{3,2,0,1:T(8,128)(2,1)S(1)} %pad_maximum_fusion), channel_id=1, source_target_pairs={{2,0},{3,1},{4,2},{5,3},{6,4},{7,5},{8,6},{9,7},{10,8},{11,9},{12,... | collective-permute-start | bytes 261128 | tf_op jit(solution)/shard_map/ppermute | solution.py:23
  51.9 40.7 %copy-start.12 = (f32[640]{0:T(1024)S(1)}, f32[640]{0:T(1024)}, u32[]{:S(2)}) copy-start(f32[640]{0:T(1024)} %param.26) | copy-start | bytes 7684
  52.0 40.7 %copy-start.13 = (f32[640]{0:T(1024)S(1)}, f32[640]{0:T(1024)}, u32[]{:S(2)}) copy-start(f32[640]{0:T(1024)} %param.25) | copy-start | bytes 7684
  93.0 3.7 %copy-start.6 = (bf16[640,640]{1,0:T(8,128)(2,1)S(1)}, bf16[640,640]{1,0:T(8,128)(2,1)}, u32[]{:S(2)}) copy-start(bf16[640,640]{1,0:T(8,128)(2,1)} %param.29) | copy-start | bytes 2457604
  97.2 3.7 %copy-start.5 = (bf16[640,640]{1,0:T(8,128)(2,1)S(1)}, bf16[640,640]{1,0:T(8,128)(2,1)}, u32[]{:S(2)}) copy-start(bf16[640,640]{1,0:T(8,128)(2,1)} %param.27) | copy-start | bytes 2457604
  101.4 3.9 %copy-start.7 = (bf16[640,640]{1,0:T(8,128)(2,1)S(1)}, bf16[640,640]{1,0:T(8,128)(2,1)}, u32[]{:S(2)}) copy-start(bf16[640,640]{1,0:T(8,128)(2,1)} %param.29) | copy-start | bytes 2457604
  101.4 3.9 %copy-start.15 = (bf16[2,16,32,640]{3,2,1,0:T(8,128)(2,1)S(1)}, bf16[2,16,32,640]{3,2,1,0:T(8,128)(2,1)}, u32[]{:S(2)}) copy-start(bf16[2,16,32,640]{3,2,1,0:T(8,128)(2,1)} %all-gather.2.cloned.1.call-done) | copy-start | bytes 3932164
  124.7 1.6 %copy-start.4 = (bf16[640,640]{1,0:T(8,128)(2,1)S(1)}, bf16[640,640]{1,0:T(8,128)(2,1)}, u32[]{:S(2)}) copy-start(bf16[640,640]{1,0:T(8,128)(2,1)} %param.30) | copy-start | bytes 2457604
  125.9 1.1 copy-start.2
  125.9 1.1 copy-start.14
  126.6 1.6 %copy-start.8 = (bf16[2,77,640]{1,2,0:T(8,128)(2,1)S(1)}, bf16[2,77,640]{1,2,0:T(8,128)(2,1)}, u32[]{:S(2)}) copy-start(bf16[2,77,640]{1,2,0:T(8,128)(2,1)} %copy.46) | copy-start | bytes 591364
  127.4 1.5 %copy-start.3 = (bf16[640,640]{1,0:T(8,128)(2,1)S(1)}, bf16[640,640]{1,0:T(8,128)(2,1)}, u32[]{:S(2)}) copy-start(bf16[640,640]{1,0:T(8,128)(2,1)} %param.33) | copy-start | bytes 2457604
Sparse Core Ops, SparseCore 0:
  9.6 41.1 all-gather.1
where the time goes:
time: 138 us; the launch traced here: 137 us
  blocking collectives  66 us (48%)
  local copies, waits for them, and re-layouts  23 us (17%)
  matrix products  15.2 us (11%)
  between operations  13.9 us (10%)
  other arithmetic  12 us (9%)
  waiting for transfers between devices  3.85 us (3%)
  starting transfers between devices  2.7 us (2%)
    psum x2, blocking collectives, group_norm(): lax.psum((jnp.sum(grouped, axis=(1, 2, 4)), jnp.sum(grouped * grouped, ax...  66 us
    select_n x1, other arithmetic, fold_pair(): piece_keys = jnp.where(mine[None, :, None, None], fresh_keys, piece_keys)  6.78 us
    dot_general x6, matrix products, project(): jnp.dot(values, weight, preferred_element_type=jnp.float32)  6.32 us
    reshape x1, local copies, waits for them, and re-layouts, fold_inputs(): project(piece_flat, key_weight).reshape(images, span, columns, width)  5.81 us
    dot_general x1, matrix products, patch_conv(): jnp.dot(taps.reshape(images * columns, 9 * channels), conv_weight.reshape...  4.5 us
    broadcast_in_dim x4, local copies, waits for them, and re-layouts, fold_pair(): piece_keys = jnp.where(mine[None, :, None, None], fresh_keys, piece_keys)  4 us
    ppermute x2, waiting for transfers between devices, shifted(): lax.ppermute(value, axis, [(source, source + steps) for source in range(i...  3.81 us
    broadcast_in_dim x2, local copies, waits for them, and re-layouts, fold_pair(): jnp.where(mine[None, :, None, None], fresh_values, piece_values)  3.81 us
  transfers between devices with their start and end apart: 4, of which 1 were waited for; matrix products, arithmetic and copies ran while one was open for 15% of the time, Pallas kernels for 0%

commit v1 on v0

v1 whole, which is shorter than its diff:
```python
import functools

import jax
import jax.numpy as jnp
from jax import lax
from jax.experimental import pallas as pl
from jax.experimental.pallas import tpu as pltpu
from jax.sharding import PartitionSpec as P

GROUPS = 32
HEADS = 10
HEAD_DIM = 64
EPSILON = 1e-05
MESH = pl.DeviceIdType.MESH
LANES = 128
F32 = jnp.float32
BF16 = jnp.bfloat16
HIGH = lax.Precision.HIGHEST


def dot(a, b, **kw):
    return jnp.dot(a, b, preferred_element_type=F32, **kw)


def dot_t(a, b):
    return lax.dot_general(a, b, (((1,), (1,)), ((), ())), preferred_element_type=F32)


def group_matrix(channels, transposed):
    width = channels // GROUPS
    shape = (LANES, channels) if transposed else (channels, LANES)
    channel = lax.broadcasted_iota(jnp.int32, shape, 1 if transposed else 0)
    group = lax.broadcasted_iota(jnp.int32, shape, 0 if transposed else 1)
    inside = (channel >= group * width) & (channel < (group + 1) * width)
    return jnp.where(inside, 1.0, 0.0).astype(F32)


def pair_attention(q, k, v, lane):
    cols = q.shape[0]
    low = lane < HEAD_DIM
    both = jnp.concatenate([jnp.where(low, q, 0.0), jnp.where(low, 0.0, q)], axis=0).astype(BF16)
    scores = dot_t(both, k)
    weights = jnp.exp(scores - jnp.max(scores, axis=-1, keepdims=True))
    totals = jnp.sum(weights, axis=-1, keepdims=True)
    out = dot(weights.astype(BF16), v) / totals
    return jnp.where(low, out[:cols], out[cols:])


def kernel(
    patches, images, cols,
    feat_h, sconv_h, snorm_h, fg_h, fb_h, wc_h, cb_h, sg_h, sb_h,
    wq_h, wk_h, wv_h, wo_h, lg_h, wcq_h, wco_h, tk_h, tv_h,
    out_ref,
    feat, sconv, xall, kall, vall, wc, ws, vec, tk, tv,
    stats, halo, edge_src, edges, lhs, hid, att,
    st_send, st_recv, xz_send, xy_send, xc_send, x_recv,
    halo_send, halo_recv, edge_send, edge_recv, in_sem, wc_sem, w_sem, v_sem,
):
    channels = feat.shape[-1]
    rows = images * cols
    outer = patches // 4
    chips = patches // 2
    me = lax.axis_index("patch")
    chip, core = me // 2, me % 2
    zo, yi = chip // 2, chip % 2
    partner = chip * 2 + (1 - core)

    def index(o, i, c):
        return (o * 2 + i) * 2 + c

    def xslot(slot):
        return xall.at[:, pl.ds(pl.multiple_of(slot * cols, cols), cols), :]

    cp_feat = pltpu.make_async_copy(feat_h, feat, in_sem.at[0])
    cp_sconv = pltpu.make_async_copy(sconv_h, sconv, in_sem.at[1])
    cp_snorm = pltpu.make_async_copy(snorm_h, xslot(me), in_sem.at[2])
    cp_tk = pltpu.make_async_copy(tk_h, tk, in_sem.at[3])
    cp_tv = pltpu.make_async_copy(tv_h, tv, in_sem.at[4])
    cp_feat.start()
    cp_sconv.start()
    cp_snorm.start()
    cp_vec = [
        pltpu.make_async_copy(h, vec.at[t], v_sem.at[t])
        for t, h in enumerate((fg_h, fb_h, cb_h, sg_h, sb_h, lg_h))
    ]
    for c in cp_vec:
        c.start()
    barrier = pltpu.get_barrier_semaphore()

    def greet(d, carry):
        pl.semaphore_signal(
            barrier, inc=1, device_id={"patch": lax.rem(me + d, patches)}, device_id_type=MESH
        )
        return carry

    row_first, row_last = chip == 0, chip == chips - 1

    @pl.when(row_first)
    def _():
        halo[0] = jnp.zeros(halo.shape[1:], BF16)
        edges[0] = jnp.zeros(edges.shape[1:], F32)

    @pl.when(row_last)
    def _():
        halo[1] = jnp.zeros(halo.shape[1:], BF16)
        edges[2] = jnp.zeros(edges.shape[1:], F32)

    lax.fori_loop(1, patches, greet, 0)
    cp_wc = {}
    for j in range(3):
        for i in range(3):
            cp_wc[i, j] = pltpu.make_async_copy(wc_h.at[i, j], wc.at[i, j], wc_sem.at[i * 3 + j])
            cp_wc[i, j].start()
    cp_w = [
        pltpu.make_async_copy(h, ws.at[t], w_sem.at[t])
        for t, h in enumerate((wk_h, wv_h, wq_h, wo_h, wcq_h, wco_h))
    ]
    for c in cp_w:
        c.start()
    cp_tk.start()
    cp_tv.start()

    gather_groups = group_matrix(channels, False)
    spread_groups = group_matrix(channels, True)
    count = float(patches * cols * (channels // GROUPS))

    def local_stats(phase, x):
        sums = [jnp.sum(x[b * cols:(b + 1) * cols], axis=0, keepdims=True) for b in range(images)]
        squares = [
            jnp.sum(x[b * cols:(b + 1) * cols] * x[b * cols:(b + 1) * cols], axis=0, keepdims=True)
            for b in range(images)
        ]
        table = jnp.concatenate(sums + squares, axis=0)
        stats[phase, me] = dot(table, gather_groups, precision=HIGH)

    def stat_copy(phase, slot, d):
        return pltpu.make_async_remote_copy(
            src_ref=stats.at[phase, slot],
            dst_ref=stats.at[phase, slot],
            send_sem=st_send.at[phase, d],
            recv_sem=st_recv.at[phase, slot],
            device_id={"patch": lax.rem(me + d, patches)},
            device_id_type=MESH,
        )

    def send_stats(phase):
        def body(d, carry):
            stat_copy(phase, me, d).start()
            return carry
        lax.fori_loop(1, patches, body, 0)

    def finish_stats(phase):
        def body(d, carry):
            stat_copy(phase, lax.rem(me + d, patches), d).wait_recv()
            return carry
        lax.fori_loop(1, patches, body, 0)
        total = jnp.sum(stats[phase], axis=0) / count
        mean = total[:images]
        var = total[images:] - mean * mean
        table = jnp.concatenate([mean, lax.rsqrt(var + EPSILON)], axis=0)
        return dot(table, spread_groups, precision=HIGH)

    def normed(x, table, b, gain, bias):
        part = x[b * cols:(b + 1) * cols]
        return (part - table[b:b + 1]) * table[images + b:images + b + 1] * gain + bias

    def x_copy(slot, target, send):
        return pltpu.make_async_remote_copy(
            src_ref=xslot(slot), dst_ref=xslot(slot), send_sem=send, recv_sem=x_recv.at[slot],
            device_id={"patch": target}, device_id_type=MESH,
        )

    def halo_copy(which, step):
        return pltpu.make_async_remote_copy(
            src_ref=sconv, dst_ref=halo.at[which], send_sem=halo_send.at[which],
            recv_sem=halo_recv.at[which],
            device_id={"patch": lax.rem(me + 2 * step + patches, patches)}, device_id_type=MESH,
        )

    def edge_copy(which, step):
        return pltpu.make_async_remote_copy(
            src_ref=edge_src, dst_ref=edges.at[which], send_sem=edge_send.at[which],
            recv_sem=edge_recv.at[which],
            device_id={"patch": lax.rem(partner + 2 * step + patches, patches)}, device_id_type=MESH,
        )

    cp_feat.wait()
    x = feat[...].reshape(rows, channels).astype(F32)
    local_stats(0, x)
    cp_sconv.wait()
    whole_conv = sconv[...].astype(F32)
    edge_src[...] = jnp.where(core == 0, whole_conv[:, cols - 1], whole_conv[:, 0])
    for c in cp_vec:
        c.wait()
    cp_snorm.wait()

    pl.semaphore_wait(barrier, patches - 1)
    send_stats(0)
    edge_copy(1, 0).start()

    @pl.when(jnp.logical_not(row_last))
    def _():
        halo_copy(0, 1).start()
        edge_copy(0, 1).start()

    @pl.when(jnp.logical_not(row_first))
    def _():
        halo_copy(1, -1).start()
        edge_copy(2, -1).start()

    x_copy(me, index(zo, 1 - yi, core), xy_send.at[0]).start()

    def z_send(d, carry):
        x_copy(me, index(lax.rem(zo + d, outer), yi, core), xz_send.at[d]).start()
        return carry

    lax.fori_loop(1, outer, z_send, 0)
    x_copy(me, partner, xc_send.at[0]).start()

    def forward_z(d, carry):
        slot = index(lax.rem(zo - d + outer, outer), yi, core)
        x_copy(slot, partner, xz_send.at[d]).wait_recv()
        x_copy(slot, index(zo, 1 - yi, core), xy_send.at[d]).start()
        x_copy(slot, partner, xc_send.at[d]).start()
        return carry

    def forward_y(d, carry):
        slot = index(lax.rem(zo - d + outer, outer), 1 - yi, core)
        x_copy(slot, partner, xz_send.at[0]).wait_recv()
        x_copy(slot, partner, xc_send.at[outer + d]).start()
        return carry

    table = finish_stats(0)
    for b in range(images):
        v = normed(x, table, b, vec[0], vec[1])
        lhs[1, b * cols:(b + 1) * cols, :] = (v * (1.0 / (1.0 + jnp.exp(-v)))).astype(BF16)

    edge_copy(1, 0).wait_recv()

    @pl.when(jnp.logical_not(row_first))
    def _():
        halo_copy(0, 1).wait_recv()
        edge_copy(0, 1).wait_recv()

    @pl.when(jnp.logical_not(row_last))
    def _():
        halo_copy(1, -1).wait_recv()
        edge_copy(2, -1).wait_recv()

    for which, row in ((0, 0), (1, 2)):
        lhs[row, :rows, :] = halo[which].reshape(rows, channels)
    filler = jnp.zeros((lhs.shape[1] - rows - images, channels), F32)
    for row in range(3):
        lhs[row, rows:, :] = jnp.concatenate([edges[row], filler], axis=0).astype(BF16)

    third = [1 + (outer - 1) * t // 3 for t in range(4)]
    parts = []
    for j in range(3):
        total = None
        for i in range(3):
            cp_wc[i, j].wait()
            term = dot(lhs[i], wc[i, j])
            total = term if total is None else total + term
        parts.append(total)
        if j < 2:
            lax.fori_loop(third[j], third[j + 1], forward_z, 0)
    place = lax.broadcasted_iota(jnp.int32, (cols, channels), 0)
    for b in range(images):
        left = pltpu.roll(parts[0][b * cols:(b + 1) * cols], 1, 0)
        right = pltpu.roll(parts[2][b * cols:(b + 1) * cols], cols - 1, 0)
        left_edge = jnp.where(core == 1, parts[0][rows + b:rows + b + 1], 0.0)
        right_edge = jnp.where(core == 0, parts[2][rows + b:rows + b + 1], 0.0)
        left = jnp.where(place == 0, left_edge, left)
        right = jnp.where(place == cols - 1, right_edge, right)
        conv = left + parts[1][b * cols:(b + 1) * cols] + right
        hid[b * cols:(b + 1) * cols, :] = x[b * cols:(b + 1) * cols] + conv + vec[2]

    hidden = hid[...]
    local_stats(1, hidden)
    send_stats(1)
    lax.fori_loop(third[2], third[3], forward_z, 0)
    lax.fori_loop(0, outer, forward_y, 0)

    def from_partner(t, carry):
        x_copy(t * 2 + (1 - core), partner, xz_send.at[0]).wait_recv()
        return carry

    lax.fori_loop(0, chips, from_partner, 0)
    cp_w[0].wait()
    cp_w[1].wait()
    span = patches * cols
    piece = min(span, 256)

    def stale_kv(t, carry):
        at = pl.ds(pl.multiple_of(t * piece, piece), piece)
        for b in range(images):
            block = xall[b, at, :]
            kall[b, at, :] = dot(block, ws[0]).astype(BF16)
            vall[b, at, :] = dot(block, ws[1]).astype(BF16)
        return carry

    lax.fori_loop(0, span // piece, stale_kv, 0)
    cp_w[2].wait()
    table = finish_stats(1)
    attn_in = jnp.concatenate(
        [normed(hidden, table, b, vec[3], vec[4]) for b in range(images)], axis=0
    ).astype(BF16)
    own = pl.ds(pl.multiple_of(me * cols, cols), cols)
    fresh_k = dot(attn_in, ws[0]).astype(BF16)
    fresh_v = dot(attn_in, ws[1]).astype(BF16)
    for b in range(images):
        kall[b, own, :] = fresh_k[b * cols:(b + 1) * cols]
        vall[b, own, :] = fresh_v[b * cols:(b + 1) * cols]
    scale = HEAD_DIM ** -0.5
    lane = lax.broadcasted_iota(jnp.int32, (cols, LANES), 1)

    def heads(q, keys, values):
        for b in range(images):
            for pair in range(channels // LANES):
                at = slice(pair * LANES, (pair + 1) * LANES)
                part = pair_attention(
                    q[b * cols:(b + 1) * cols, at], keys[b, :, at], values[b, :, at], lane
                )
                att[b * cols:(b + 1) * cols, at] = part.astype(BF16)

    heads(dot(attn_in, ws[2]).astype(BF16).astype(F32) * scale, kall, vall)
    cp_w[3].wait()
    mixed = hidden + dot(att[...], ws[3])
    centred = mixed - jnp.mean(mixed, axis=-1, keepdims=True)
    variance = jnp.mean(centred * centred, axis=-1, keepdims=True)
    layer_in = (centred * lax.rsqrt(variance + EPSILON) * vec[5]).astype(BF16)
    cp_w[4].wait()
    cp_tk.wait()
    cp_tv.wait()
    heads(dot(layer_in, ws[4]).astype(BF16).astype(F32) * scale, tk, tv)
    cp_w[5].wait()
    out_ref[...] = (mixed + dot(att[...], ws[5])).reshape(images, 1, cols, channels)

    def drain_stats(d, carry):
        stat_copy(0, me, d).wait_send()
        stat_copy(1, me, d).wait_send()
        return carry

    lax.fori_loop(1, patches, drain_stats, 0)

    def drain_z(d, carry):
        x_copy(me, partner, xz_send.at[d]).wait_send()
        return carry

    lax.fori_loop(1, outer, drain_z, 0)

    def drain_y(d, carry):
        x_copy(me, partner, xy_send.at[d]).wait_send()
        return carry

    lax.fori_loop(0, outer, drain_y, 0)

    def drain_c(d, carry):
        x_copy(me, partner, xc_send.at[d]).wait_send()
        return carry

    lax.fori_loop(0, chips, drain_c, 0)
    edge_copy(1, 0).wait_send()

    @pl.when(jnp.logical_not(row_last))
    def _():
        halo_copy(0, 1).wait_send()
        edge_copy(0, 1).wait_send()

    @pl.when(jnp.logical_not(row_first))
    def _():
        halo_copy(1, -1).wait_send()
        edge_copy(2, -1).wait_send()


def solution(mesh):
    patches = mesh.shape["patch"]

    def on_device(
        features, stale_conv_in, stale_normed, first_gain, first_bias, conv_weight, conv_bias,
        second_gain, second_bias, query_weight, key_weight, value_weight, output_weight,
        layer_gain, cross_query, cross_output, text_keys, text_values,
    ):
        images, _, cols, channels = features.shape
        rows = images * cols
        span = patches * cols
        outer = patches // 4

        def flat(a):
            return a.reshape(images, cols, channels)

        def row(a):
            return a.reshape(1, channels)

        dma = pltpu.SemaphoreType.DMA
        return pl.pallas_call(
            functools.partial(kernel, patches, images, cols),
            out_shape=jax.ShapeDtypeStruct(features.shape, F32),
            in_specs=[pl.BlockSpec(memory_space=pl.ANY)] * 18,
            out_specs=pl.BlockSpec(memory_space=pltpu.VMEM),
            scratch_shapes=[
                pltpu.VMEM((images, cols, channels), BF16),
                pltpu.VMEM((images, cols, channels), BF16),
                pltpu.VMEM((images, span, channels), BF16),
                pltpu.VMEM((images, span, channels), BF16),
                pltpu.VMEM((images, span, channels), BF16),
                pltpu.VMEM(conv_weight.shape, BF16),
                pltpu.VMEM((6, channels, channels), BF16),
                pltpu.VMEM((6, 1, channels), F32),
                pltpu.VMEM(text_keys.shape, BF16),
                pltpu.VMEM(text_values.shape, BF16),
                pltpu.VMEM((2, patches, 2 * images, LANES), F32),
                pltpu.VMEM((2, images, cols, channels), BF16),
                pltpu.VMEM((images, channels), F32),
                pltpu.VMEM((3, images, channels), F32),
                pltpu.VMEM((3, rows + 16, channels), BF16),
                pltpu.VMEM((rows, channels), F32),
                pltpu.VMEM((rows, channels), BF16),
                dma((2, patches)), dma((2, patches)),
                dma((outer,)), dma((outer,)), dma((2 * outer,)), dma((patches,)),
                dma((2,)), dma((2,)), dma((3,)), dma((3,)),
                dma((5,)), dma((9,)), dma((6,)), dma((6,)),
            ],
            compiler_params=pltpu.CompilerParams(
                collective_id=0, has_side_effects=True, vmem_limit_bytes=63000 * 1024
            ),
        )(
            flat(features), flat(stale_conv_in), flat(stale_normed), row(first_gain),
            row(first_bias), conv_weight, row(conv_bias), row(second_gain), row(second_bias),
            query_weight, key_weight, value_weight, output_weight, row(layer_gain),
            cross_query, cross_output, text_keys, text_values,
        )

    act = P("grp", "patch", None, None)
    text = P("grp", None, None)
    return jax.shard_map(
        on_device, mesh=mesh,
        in_specs=(act,) * 3 + (P(),) * 13 + (text,) * 2,
        out_specs=act, check_vma=False,
    )
```

time: 138 us -> 45.9 us (0.33)
  blocking collectives: 66 us -> 0 us
  Pallas kernels: 0 us -> 33 us
  matrix products: 15.2 us -> 0 us
  between operations: 13.9 us -> 0.01 us
  other arithmetic: 12 us -> 0 us
  local copies, waits for them, and re-layouts: 23 us -> 12.5 us
  waiting for transfers between devices: 3.85 us -> 0 us
  starting transfers between devices: 2.7 us -> 0 us
    psum x2 -> x0, blocking collectives: 66 us -> none  [group_norm(): lax.psum((jnp.sum(grouped, axis=(1, 2, 4)), jnp.sum(grouped * grouped, ax...]
    pallas_call x0 -> x1, Pallas kernels: none -> 33 us  [on_device(): pl.pallas_call(functools.partial(kernel, patches, images, cols), out_shap...]
    dot_general x13 -> x0, matrix products: 15.2 us -> none  [the longest x6 6.32 us: project(): jnp.dot(values, weight, preferred_element_type=jnp.float32)]
    broadcast_in_dim x6 -> x0, local copies, waits for them, and re-layouts: 7.81 us -> none  [the longest x4 4 us: fold_pair(): piece_keys = jnp.where(mine[None, :, None, None], fresh_keys, piece_keys)]
    select_n x3 -> x0, other arithmetic: 7.63 us -> none  [the longest x1 6.78 us: fold_pair(): piece_keys = jnp.where(mine[None, :, None, None], fresh_keys, piece_keys)]
    ppermute x3 -> x0, waiting for transfers between devices: 3.81 us -> none  [the longest x2 3.81 us: shifted(): lax.ppermute(value, axis, [(source, source + steps) for source in range(i...]
    ppermute x3 -> x0, starting transfers between devices: 2.66 us -> none  [the longest x2 2.58 us: shifted(): lax.ppermute(value, axis, [(source, source + steps) for source in range(i...]
    reshape x4 -> x6, local copies, waits for them, and re-layouts: 9.92 us -> 7.63 us  [row(): return a.reshape(1, channels)]
  transfers between devices with their start and end apart: 4 -> 0, of which waited for: 1 -> 0; matrix products, arithmetic and copies ran while one was open for 15% -> 0% of each run, Pallas kernels for 0% -> 0%
where the time goes in v1:
time: 45.9 us; the launch traced here: 45.5 us
  Pallas kernels  33 us (72%)
  local copies, waits for them, and re-layouts  12.5 us (27%)
    pallas_call x1, Pallas kernels, on_device(): pl.pallas_call(functools.partial(kernel, patches, images, cols), out_shap...  33 us
    reshape x6, local copies, waits for them, and re-layouts, row(): return a.reshape(1, channels)  7.63 us
    unnamed x3, local copies, waits for them, and re-layouts  4.84 us

profile of v1, /device:TPU:1, one launch (start us, length us, event | category | flops | bytes accessed | tf_op | source)
XLA Modules:
  0.0 45.5 jit_solution(18405771169724891324)
XLA Ops:
  0.0 1.3 %reshape.30.fg_h = f32[1,640]{1,0:T(1,128)} reshape(f32[640]{0:T(1024)} %param.21) | data formatting | bytes 5120 | tf_op jit(solution)/shard_map/reshape | solution.py:393
  1.3 1.3 %reshape.31.fb_h = f32[1,640]{1,0:T(1,128)} reshape(f32[640]{0:T(1024)} %param.22) | data formatting | bytes 5120 | tf_op jit(solution)/shard_map/reshape | solution.py:393
  2.5 1.3 %reshape.32.cb_h = f32[1,640]{1,0:T(1,128)} reshape(f32[640]{0:T(1024)} %param.24) | data formatting | bytes 5120 | tf_op jit(solution)/shard_map/reshape | solution.py:393
  3.8 1.3 %reshape.33.sg_h = f32[1,640]{1,0:T(1,128)} reshape(f32[640]{0:T(1024)} %param.25) | data formatting | bytes 5120 | tf_op jit(solution)/shard_map/reshape | solution.py:393
  5.1 1.3 %reshape.34.sb_h = f32[1,640]{1,0:T(1,128)} reshape(f32[640]{0:T(1024)} %param.26) | data formatting | bytes 5120 | tf_op jit(solution)/shard_map/reshape | solution.py:393
  6.4 1.3 %reshape.35.lg_h = f32[1,640]{1,0:T(1,128)} reshape(f32[640]{0:T(1024)} %param.31) | data formatting | bytes 5120 | tf_op jit(solution)/shard_map/reshape | solution.py:393
  7.6 1.6 %copy.19.tk_h = bf16[2,77,640]{2,1,0:T(8,128)(2,1)} copy(bf16[2,77,640]{2,0,1:T(2,128)(2,1)} %param.34) | data formatting | bytes 394240 | tf_op args[16]
  9.3 1.6 %copy.20.tv_h = bf16[2,77,640]{2,1,0:T(8,128)(2,1)} copy(bf16[2,77,640]{2,0,1:T(2,128)(2,1)} %param.35) | data formatting | bytes 394240 | tf_op args[17]
  10.9 33.0 %shard_map.172 = f32[2,1,32,640]{3,2,1,0:T(8,128)} custom-call(bf16[2,32,640]{2,1,0:T(8,128)(2,1)} %bitcast.3, bf16[2,32,640]{2,1,0:T(8,128)(2,1)} %bitcast.4, bf16[2,32,640]{2,1,0:T(8,128)(2,1)} %bitcast.5, f32[1,640]{1,0:T(1,128)} %reshape.30.fg_h, f32[1,640]{1,0:T(1,128)} %reshape.31.fb_h, bf16[3,3,640,640]{3,2,1,0:T(8,128)(2,1)} %wc_h.1, ...), custom_call_target="tpu_custom_call" | custom-call | tf_op jit(solution)/shard_map/pallas_call | solution.py:396
  43.9 1.6 %copy.22 = f32[2,1,32,640]{3,2,1,0:T(8,128)} copy(f32[2,1,32,640]{3,2,1,0:T(8,128)} %shard_map.172) | data formatting | bytes 327680

commit v2 on v1

--- a/solution.py
+++ b/solution.py
@@ -18,6 +18,10 @@
 HIGH = lax.Precision.HIGHEST
 
 
+def mark(name):
+    pass
+
+
 def dot(a, b, **kw):
     return jnp.dot(a, b, preferred_element_type=F32, **kw)
 
@@ -49,9 +53,9 @@
 def kernel(
     patches, images, cols,
     feat_h, sconv_h, snorm_h, fg_h, fb_h, wc_h, cb_h, sg_h, sb_h,
-    wq_h, wk_h, wv_h, wo_h, lg_h, wcq_h, wco_h, tk_h, tv_h,
-    out_ref,
-    feat, sconv, xall, kall, vall, wc, ws, vec, tk, tv,
+    wq_h, wk_h, wv_h, wo_h, lg_h, wcq_h, tk_h, tv_h,
+    mixed_ref, att_ref,
+    feat, sconv, xall, kall, vall, wc, ws, v0, v1, v2, v3, v4, v5, tk_in, tv_in, tk, tv,
     stats, halo, edge_src, edges, lhs, hid, att,
     st_send, st_recv, xz_send, xy_send, xc_send, x_recv,
     halo_send, halo_recv, edge_send, edge_recv, in_sem, wc_sem, w_sem, v_sem,
@@ -74,14 +78,14 @@
     cp_feat = pltpu.make_async_copy(feat_h, feat, in_sem.at[0])
     cp_sconv = pltpu.make_async_copy(sconv_h, sconv, in_sem.at[1])
     cp_snorm = pltpu.make_async_copy(snorm_h, xslot(me), in_sem.at[2])
-    cp_tk = pltpu.make_async_copy(tk_h, tk, in_sem.at[3])
-    cp_tv = pltpu.make_async_copy(tv_h, tv, in_sem.at[4])
+    cp_tk = pltpu.make_async_copy(tk_h, tk_in, in_sem.at[3])
+    cp_tv = pltpu.make_async_copy(tv_h, tv_in, in_sem.at[4])
     cp_feat.start()
     cp_sconv.start()
     cp_snorm.start()
     cp_vec = [
-        pltpu.make_async_copy(h, vec.at[t], v_sem.at[t])
-        for t, h in enumerate((fg_h, fb_h, cb_h, sg_h, sb_h, lg_h))
+        pltpu.make_async_copy(h, own_vec, v_sem.at[t])
+        for t, (h, own_vec) in enumerate(zip((fg_h, fb_h, cb_h, sg_h, sb_h, lg_h), (v0, v1, v2, v3, v4, v5)))
     ]
     for c in cp_vec:
         c.start()
@@ -113,7 +117,7 @@
             cp_wc[i, j].start()
     cp_w = [
         pltpu.make_async_copy(h, ws.at[t], w_sem.at[t])
-        for t, h in enumerate((wk_h, wv_h, wq_h, wo_h, wcq_h, wco_h))
+        for t, h in enumerate((wk_h, wv_h, wq_h, wo_h, wcq_h))
     ]
     for c in cp_w:
         c.start()
@@ -184,17 +188,22 @@
             device_id={"patch": lax.rem(partner + 2 * step + patches, patches)}, device_id_type=MESH,
         )
 
+    mark("stats0")
     cp_feat.wait()
     x = feat[...].reshape(rows, channels).astype(F32)
     local_stats(0, x)
+    mark("edges")
     cp_sconv.wait()
     whole_conv = sconv[...].astype(F32)
     edge_src[...] = jnp.where(core == 0, whole_conv[:, cols - 1], whole_conv[:, 0])
     for c in cp_vec:
         c.wait()
+    vec = [v[...].reshape(1, channels) for v in (v0, v1, v2, v3, v4, v5)]
     cp_snorm.wait()
 
+    mark("barrier")
     pl.semaphore_wait(barrier, patches - 1)
+    mark("sends")
     send_stats(0)
     edge_copy(1, 0).start()
 
@@ -230,11 +239,20 @@
         x_copy(slot, partner, xc_send.at[outer + d]).start()
         return carry
 
+    mark("text")
+    cp_tk.wait()
+    cp_tv.wait()
+    for b in range(images):
+        tk[b] = tk_in[:, b, :]
+        tv[b] = tv_in[:, b, :]
+    mark("wait0")
     table = finish_stats(0)
+    mark("norm0")
     for b in range(images):
         v = normed(x, table, b, vec[0], vec[1])
         lhs[1, b * cols:(b + 1) * cols, :] = (v * (1.0 / (1.0 + jnp.exp(-v)))).astype(BF16)
 
+    mark("halo_wait")
     edge_copy(1, 0).wait_recv()
 
     @pl.when(jnp.logical_not(row_first))
@@ -247,15 +265,18 @@
         halo_copy(1, -1).wait_recv()
         edge_copy(2, -1).wait_recv()
 
+    mark("lhs")
     for which, row in ((0, 0), (1, 2)):
         lhs[row, :rows, :] = halo[which].reshape(rows, channels)
     filler = jnp.zeros((lhs.shape[1] - rows - images, channels), F32)
     for row in range(3):
         lhs[row, rows:, :] = jnp.concatenate([edges[row], filler], axis=0).astype(BF16)
 
+    mark("conv")
     third = [1 + (outer - 1) * t // 3 for t in range(4)]
     parts = []
     for j in range(3):
+        mark(f"conv{j}")
         total = None
         for i in range(3):
             cp_wc[i, j].wait()
@@ -263,7 +284,9 @@
             total = term if total is None else total + term
         parts.append(total)
         if j < 2:
+            mark(f"fwd{j}")
             lax.fori_loop(third[j], third[j + 1], forward_z, 0)
+    mark("shift")
     place = lax.broadcasted_iota(jnp.int32, (cols, channels), 0)
     for b in range(images):
         left = pltpu.roll(parts[0][b * cols:(b + 1) * cols], 1, 0)
@@ -275,17 +298,22 @@
         conv = left + parts[1][b * cols:(b + 1) * cols] + right
         hid[b * cols:(b + 1) * cols, :] = x[b * cols:(b + 1) * cols] + conv + vec[2]
 
+    mark("stats1")
     hidden = hid[...]
     local_stats(1, hidden)
+    mark("send1")
     send_stats(1)
     lax.fori_loop(third[2], third[3], forward_z, 0)
+    mark("fwd_y")
     lax.fori_loop(0, outer, forward_y, 0)
 
     def from_partner(t, carry):
         x_copy(t * 2 + (1 - core), partner, xz_send.at[0]).wait_recv()
         return carry
 
+    mark("partner")
     lax.fori_loop(0, chips, from_partner, 0)
+    mark("kv")
     cp_w[0].wait()
     cp_w[1].wait()
     span = patches * cols
@@ -300,8 +328,10 @@
         return carry
 
     lax.fori_loop(0, span // piece, stale_kv, 0)
+    mark("wait1")
     cp_w[2].wait()
     table = finish_stats(1)
+    mark("norm1")
     attn_in = jnp.concatenate(
         [normed(hidden, table, b, vec[3], vec[4]) for b in range(images)], axis=0
     ).astype(BF16)
@@ -311,6 +341,7 @@
     for b in range(images):
         kall[b, own, :] = fresh_k[b * cols:(b + 1) * cols]
         vall[b, own, :] = fresh_v[b * cols:(b + 1) * cols]
+    mark("q")
     scale = HEAD_DIM ** -0.5
     lane = lax.broadcasted_iota(jnp.int32, (cols, LANES), 1)
 
@@ -324,18 +355,19 @@
                 att[b * cols:(b + 1) * cols, at] = part.astype(BF16)
 
     heads(dot(attn_in, ws[2]).astype(BF16).astype(F32) * scale, kall, vall)
+    mark("out_ln")
     cp_w[3].wait()
     mixed = hidden + dot(att[...], ws[3])
     centred = mixed - jnp.mean(mixed, axis=-1, keepdims=True)
     variance = jnp.mean(centred * centred, axis=-1, keepdims=True)
     layer_in = (centred * lax.rsqrt(variance + EPSILON) * vec[5]).astype(BF16)
+    mark("cross")
     cp_w[4].wait()
-    cp_tk.wait()
-    cp_tv.wait()
     heads(dot(layer_in, ws[4]).astype(BF16).astype(F32) * scale, tk, tv)
-    cp_w[5].wait()
-    out_ref[...] = (mixed + dot(att[...], ws[5])).reshape(images, 1, cols, channels)
-
+    att_ref[...] = att[...]
+    mixed_ref[...] = mixed
+
+    mark("drain")
     def drain_stats(d, carry):
         stat_copy(0, me, d).wait_send()
         stat_copy(1, me, d).wait_send()
@@ -385,19 +417,20 @@
         rows = images * cols
         span = patches * cols
         outer = patches // 4
+        ctx = text_keys.shape[1]
 
         def flat(a):
             return a.reshape(images, cols, channels)
 
-        def row(a):
-            return a.reshape(1, channels)
-
         dma = pltpu.SemaphoreType.DMA
-        return pl.pallas_call(
+        mixed, attended = pl.pallas_call(
             functools.partial(kernel, patches, images, cols),
-            out_shape=jax.ShapeDtypeStruct(features.shape, F32),
-            in_specs=[pl.BlockSpec(memory_space=pl.ANY)] * 18,
-            out_specs=pl.BlockSpec(memory_space=pltpu.VMEM),
+            out_shape=(
+                jax.ShapeDtypeStruct((rows, channels), F32),
+                jax.ShapeDtypeStruct((rows, channels), BF16),
+            ),
+            in_specs=[pl.BlockSpec(memory_space=pl.ANY)] * 17,
+            out_specs=(pl.BlockSpec(memory_space=pltpu.VMEM),) * 2,
             scratch_shapes=[
                 pltpu.VMEM((images, cols, channels), BF16),
                 pltpu.VMEM((images, cols, channels), BF16),
@@ -405,10 +438,12 @@
                 pltpu.VMEM((images, span, channels), BF16),
                 pltpu.VMEM((images, span, channels), BF16),
                 pltpu.VMEM(conv_weight.shape, BF16),
-                pltpu.VMEM((6, channels, channels), BF16),
-                pltpu.VMEM((6, 1, channels), F32),
-                pltpu.VMEM(text_keys.shape, BF16),
-                pltpu.VMEM(text_values.shape, BF16),
+                pltpu.VMEM((5, channels, channels), BF16),
+                *[pltpu.VMEM((channels,), F32)] * 6,
+                pltpu.VMEM((ctx, images, channels), BF16),
+                pltpu.VMEM((ctx, images, channels), BF16),
+                pltpu.VMEM((images, ctx, channels), BF16),
+                pltpu.VMEM((images, ctx, channels), BF16),
                 pltpu.VMEM((2, patches, 2 * images, LANES), F32),
                 pltpu.VMEM((2, images, cols, channels), BF16),
                 pltpu.VMEM((images, channels), F32),
@@ -419,17 +454,18 @@
                 dma((2, patches)), dma((2, patches)),
                 dma((outer,)), dma((outer,)), dma((2 * outer,)), dma((patches,)),
                 dma((2,)), dma((2,)), dma((3,)), dma((3,)),
-                dma((5,)), dma((9,)), dma((6,)), dma((6,)),
+                dma((5,)), dma((9,)), dma((5,)), dma((6,)),
             ],
             compiler_params=pltpu.CompilerParams(
                 collective_id=0, has_side_effects=True, vmem_limit_bytes=63000 * 1024
             ),
         )(
-            flat(features), flat(stale_conv_in), flat(stale_normed), row(first_gain),
-            row(first_bias), conv_weight, row(conv_bias), row(second_gain), row(second_bias),
-            query_weight, key_weight, value_weight, output_weight, row(layer_gain),
-            cross_query, cross_output, text_keys, text_values,
-        )
+            flat(features), flat(stale_conv_in), flat(stale_normed), first_gain, first_bias,
+            conv_weight, conv_bias, second_gain, second_bias, query_weight, key_weight,
+            value_weight, output_weight, layer_gain, cross_query,
+            text_keys.transpose(1, 0, 2), text_values.transpose(1, 0, 2),
+        )
+        return (mixed + dot(attended, cross_output)).reshape(features.shape)
 
     act = P("grp", "patch", None, None)
     text = P("grp", None, None)

time: 45.9 us -> 34.8 us (0.76)
  local copies, waits for them, and re-layouts: 12.5 us -> 0.01 us
  matrix products: 0 us -> 1.89 us
    reshape x6 -> x0, local copies, waits for them, and re-layouts: 7.63 us -> none  [row(): return a.reshape(1, channels)]
    unnamed x3 -> x2, local copies, waits for them, and re-layouts: 4.84 us -> 0.01 us
    dot_general x0 -> x1, matrix products: none -> 1.89 us  [dot(): return jnp.dot(a, b, preferred_element_type=F32, **kw)]
where the time goes in v2:
time: 34.8 us; the launch traced here: 34.7 us
  Pallas kernels  32.8 us (94%)
  matrix products  1.89 us (5%)
    pallas_call x1, Pallas kernels, on_device(): pl.pallas_call(functools.partial(kernel, patches, images, cols), out_shap...  32.8 us
    dot_general x1, matrix products, dot(): return jnp.dot(a, b, preferred_element_type=F32, **kw)  1.89 us

profile of v2, /device:TPU:1, one launch (start us, length us, event | category | flops | bytes accessed | tf_op | source)
XLA Modules:
  0.0 34.7 jit_solution(1483315714968180900)
XLA Ops:
  0.0 0.0 copy-start
  0.0 32.8 %shard_map.172 = (f32[64,640]{1,0:T(8,128)}, bf16[64,640]{1,0:T(8,128)(2,1)}) custom-call(bf16[2,32,640]{2,1,0:T(8,128)(2,1)} %bitcast.12, bf16[2,32,640]{2,1,0:T(8,128)(2,1)} %bitcast.13, bf16[2,32,640]{2,1,0:T(8,128)(2,1)} %bitcast.14, f32[640]{0:T(1024)} %fg_h.1, f32[640]{0:T(1024)} %fb_h.1, bf16[3,3,640,640]{3,2,1,0:T(8,128)(2,1)} %wc_h.1, f32[640]{0:T(1024)} %cb_h.1, ...), custom_call_target="tpu_custom_call" | custom-call | tf_op jit(solution)/shard_map/pallas_call | solution.py:426
  32.8 0.0 copy-done
  32.8 1.9 %convolution_add_fusion = f32[64,640]{1,0:T(8,128)} fusion(f32[64,640]{1,0:T(8,128)} %get-tuple-element.7, bf16[64,640]{1,0:T(8,128)(2,1)} %get-tuple-element.8, bf16[640,640]{1,0:T(8,128)(2,1)S(1)} %copy-done), kind=kOutput, calls=%fused_computation | convolution fusion | flops 52469760 | bytes 1228800 | tf_op jit(solution)/shard_map/dot_general | solution.py:26
Async XLA Ops:
  0.0 32.8 %copy-start = (bf16[640,640]{1,0:T(8,128)(2,1)S(1)}, bf16[640,640]{1,0:T(8,128)(2,1)}, u32[]{:S(2)}) copy-start(bf16[640,640]{1,0:T(8,128)(2,1)} %param.33) | copy-start | bytes 2457604
